TPU v7x, 32 devices: a whole 2x2x4 slice. The times are simulated.
32 devices in a mesh: level: 4 (over z), dev: 8 (over y, x, core).
Axes of the slice: x: 2, y: 2, z: 4, core: 2. Of those that a mesh axis runs over, the one named last changes fastest.
Arguments:
- fields: float32 [4, 128, 12, 128], P('level', 'dev'), may hold values from -6 to 6
- own_src: int32 [4, 128], P('level', 'dev'), may hold values from 0 to 15
- own_weight: bfloat16 [4, 128, 128, 128], P('level', 'dev'), may hold values from 0 to 1, as said below
- send_block: int32 [4, 8, 8, 2], P('level', 'dev'), may hold values from 0 to 15
- send_target: int32 [4, 8, 8, 2], P('level', 'dev'), may hold values from 0 to 15
- send_count: int32 [4, 8, 8], P('level', 'dev'), may hold values from 0 to 2, as said below
- send_weight: bfloat16 [4, 8, 8, 2, 128, 128], P('level', 'dev'), may hold values from 0 to 1, as said below
- left_block: int32 [4, 8, 4, 2], P('level', 'dev'), may hold values from 0 to 15
- left_target: int32 [4, 8, 4, 2], P('level', 'dev'), may hold values from 0 to 15
- left_count: int32 [4, 8, 4], P('level', 'dev'), may hold values from 0 to 2, as said below
- left_weight: bfloat16 [4, 8, 4, 2, 128, 128], P('level', 'dev'), may hold values from 0 to 1, as said below
Outputs:
- remapped: float32 [4, 128, 12, 128], P('level', 'dev')
- totals: float32 [12], replicated
Inputs may be any that keep to these rules, and one draw needn't show every extreme that they name: send_count[l, s, s] = 0; for every level some receiver device gets 2 live slots from every other device of the level. left_count[m, q, m] = 0; for every device index some receiver level gets 2 live slots from every other level. `own_weight`: nonnegative; entry [k, i] is zero where old cell k and new cell i differ by more than 3; each column sums to a positive intersect fraction of at most 1. `send_weight`: nonnegative; entry [k, i] is zero where old cell k and new cell i differ by more than 3; each column sums to a positive intersect fraction of at most 1. `left_weight`: nonnegative; entry [k, i] is zero where old cell k and new cell i differ by more than 3; each column sums to a positive intersect fraction of at most 1.
All inputs are finite; a program needn't handle non-finite values.
Results may differ from a plain program's by a relative error of at most 0.0045.
Values may be sent and summed in bfloat16 or wider, within the bound.
A program may use at most 64 MiB of HBM per device.

v0:
```python
import jax
import jax.numpy as jnp
from jax import lax
from jax.sharding import PartitionSpec as P


def pick_donors(rounded, block_index, count):
    donors = rounded[block_index]
    slots = block_index.shape[1]
    valid = lax.broadcasted_iota(jnp.int32, (1, slots), 1) < count[:, None]
    return jnp.where(valid[:, :, None, None], donors, jnp.zeros_like(donors))


def apply_weights(donors, weights):
    return jnp.einsum("pcmk,pcki->pcmi", donors, weights, preferred_element_type=jnp.float32)


def place_terms(contrib, target, blocks):
    comp = contrib.shape[2]
    cells = contrib.shape[3]
    flat_target = target.reshape(-1)
    onehot = (flat_target[:, None] == lax.broadcasted_iota(jnp.int32, (1, blocks), 1)).astype(
        jnp.float32
    )
    return jnp.einsum(
        "sb,smi->bmi", onehot, contrib.reshape(-1, comp, cells), precision=lax.Precision.HIGHEST
    )


def body(
    fields,
    own_src,
    own_weight,
    send_block,
    send_target,
    send_count,
    send_weight,
    left_block,
    left_target,
    left_count,
    left_weight,
):
    local = fields[0]
    blocks = local.shape[0]
    rounded = local.astype(jnp.bfloat16)
    own = jnp.einsum(
        "bmk,bki->bmi", rounded[own_src[0]], own_weight[0], preferred_element_type=jnp.float32
    )
    donors = pick_donors(rounded, send_block[0, 0], send_count[0, 0])
    strays = pick_donors(rounded, left_block[0, 0], left_count[0, 0])
    intra_terms, intra_target = (
        lax.all_to_all(
            apply_weights(donors, send_weight[0, 0]), "dev", split_axis=0, concat_axis=0, tiled=True
        ),
        lax.all_to_all(send_target[0, 0], "dev", split_axis=0, concat_axis=0, tiled=True),
    )
    left_terms, left_where = (
        lax.all_to_all(
            apply_weights(strays, left_weight[0, 0]),
            "level",
            split_axis=0,
            concat_axis=0,
            tiled=True,
        ),
        lax.all_to_all(left_target[0, 0], "level", split_axis=0, concat_axis=0, tiled=True),
    )
    remapped = (
        own
        + place_terms(intra_terms, intra_target, blocks)
        + place_terms(left_terms, left_where, blocks)
    )
    sums = lax.psum(jnp.sum(remapped, axis=(0, 2)), ("level", "dev"))
    totals = sums / (remapped.shape[2] * blocks)
    return (remapped[None], totals)


def solution(mesh):
    in_specs = (
        P("level", "dev", None, None),
        P("level", "dev"),
        P("level", "dev", None, None),
        P("level", "dev", None, None),
        P("level", "dev", None, None),
        P("level", "dev", None),
        P("level", "dev", None, None, None, None),
        P("level", "dev", None, None),
        P("level", "dev", None, None),
        P("level", "dev", None),
        P("level", "dev", None, None, None, None),
    )
    out_specs = (P("level", "dev", None, None), P())
    return jax.shard_map(body, mesh=mesh, in_specs=in_specs, out_specs=out_specs, check_vma=False)
```

profile of v0, /device:TPU:0, one launch (start us, length us, event | category | flops | bytes accessed | tf_op | source)
XLA Modules:
  0.0 84.1 jit_solution(18198775144529475194)
XLA Ops:
  0.6 0.0 copy-start
  0.6 0.0 copy-start.3
  0.7 0.0 copy-start.2
  0.7 0.0 copy-start.1
  0.7 0.7 copy-done.3
  1.4 0.6 copy.41
  2.0 6.3 %all-to-all-start.2 = ((s32[4,1,2]{2,1,0:T(1,128)}), s32[4,1,2]{2,1,0:T(1,128)S(1)}, u32[]{:S(2)}, u32[]{:S(2)}) async-start(s32[4,1,2]{2,1,0:T(1,128)} %copy.41), calls=%async_computation.2 | async-start | bytes 4096 | tf_op jit(solution)/shard_map/all_to_all | solution.py:65
  8.4 0.7 fusion.21
  9.0 0.7 iota_compare_fusion.3
  9.8 0.7 compare_select_fusion.1
  10.4 0.7 iota_compare_fusion.2
  11.2 0.7 compare_select_fusion
  11.9 0.1 copy.42
  11.9 0.1 reshape.173
  12.0 0.1 copy.37
  12.1 0.1 reshape.165
  12.2 1.3 %copy.36 = s32[8,1,2]{2,1,0:T(1,128)} copy(s32[8,1,2]{0,2,1:T(2,128)} %bitcast.53) | data formatting | bytes 128 | tf_op jit(solution)/shard_map/all_to_all | solution.py:55
  13.6 0.9 %copy.52 = bf16[1,16,12,128]{3,2,1,0:T(8,128)(2,1)S(1)} copy(f32[1,16,12,128]{3,1,2,0:T(8,128)} %param.11) | data formatting | bytes 147456 | tf_op args[0]
  14.5 0.6 gather_fusion.2
  15.1 0.6 gather_fusion.1
  15.6 0.0 copy-done.2
  15.6 0.2 fusion.4
  15.9 0.0 copy-done.1
  15.9 0.3 fusion.1
  16.2 0.0 all-to-all-done.2
  16.2 3.7 %all-to-all-start = ((s32[8,1,2]{2,1,0:T(1,128)}), s32[8,1,2]{2,1,0:T(1,128)S(1)}, u32[]{:S(2)}, u32[]{:S(2)}) async-start(s32[8,1,2]{2,1,0:T(1,128)} %copy.36), calls=%async_computation | async-start | bytes 8192 | tf_op jit(solution)/shard_map/all_to_all | solution.py:55
  19.9 0.6 copy.43
  20.6 4.0 %all-to-all-done = s32[8,1,2]{2,1,0:T(1,128)S(1)} async-done(((s32[8,1,2]{2,1,0:T(1,128)}), s32[8,1,2]{2,1,0:T(1,128)S(1)}, u32[]{:S(2)}, u32[]{:S(2)}) %all-to-all-start) | async-done | bytes 96 | tf_op jit(solution)/shard_map/all_to_all | solution.py:55
  24.5 5.1 %all-to-all-start.3 = ((f32[4,2,12,128]{3,1,2,0:T(2,128)}), f32[4,2,12,128]{3,1,2,0:T(2,128)S(1)}, u32[]{:S(2)}, u32[]{:S(2)}) async-start(f32[4,2,12,128]{3,1,2,0:T(2,128)} %copy.43), calls=%async_computation.3 | async-start | bytes 98304 | tf_op jit(solution)/shard_map/all_to_all | solution.py:58
  29.6 0.6 gather_fusion
  30.2 0.7 copy.38
  30.9 0.5 broadcast.122
  31.4 0.7 reduce.6
  32.1 0.1 eq.34
  32.2 0.7 reduce.7
  32.8 0.1 eq.30
  32.9 2.4 %all-to-all-done.3 = f32[4,2,12,128]{3,1,2,0:T(2,128)S(1)} async-done(((f32[4,2,12,128]{3,1,2,0:T(2,128)}), f32[4,2,12,128]{3,1,2,0:T(2,128)S(1)}, u32[]{:S(2)}, u32[]{:S(2)}) %all-to-all-start.3) | async-done | bytes 49184 | tf_op jit(solution)/shard_map/all_to_all | solution.py:58
  35.3 3.4 %all-to-all-start.1 = ((f32[8,2,12,128]{3,1,2,0:T(2,128)}), f32[8,2,12,128]{3,1,2,0:T(2,128)S(1)}, u32[]{:S(2)}, u32[]{:S(2)}) async-start(f32[8,2,12,128]{3,1,2,0:T(2,128)} %copy.38), calls=%async_computation.1 | async-start | bytes 196608 | tf_op jit(solution)/shard_map/all_to_all | solution.py:52
  38.7 0.3 fusion.18
  39.0 4.8 %all-to-all-done.1 = f32[8,2,12,128]{3,1,2,0:T(2,128)S(1)} async-done(((f32[8,2,12,128]{3,1,2,0:T(2,128)}), f32[8,2,12,128]{3,1,2,0:T(2,128)S(1)}, u32[]{:S(2)}, u32[]{:S(2)}) %all-to-all-start.1) | async-done | bytes 98336 | tf_op jit(solution)/shard_map/all_to_all | solution.py:52
  43.9 0.2 fusion.14
  44.1 0.0 copy-done
  44.1 0.4 fusion.24
  44.4 38.5 %psum.7 = f32[12]{0:T(128)S(1)} all-reduce(f32[12]{0:T(128)S(1)} %get-tuple-element.8), channel_id=1, replica_groups=mesh['level'=4,'dev'=8] {'level','dev'}, use_global_device_ids=true, to_apply=%region_1.2 | all-reduce | flops 12 | bytes 96 | tf_op jit(solution)/shard_map/psum | solution.py:72
  82.9 0.5 broadcast_multiply_fusion
  83.4 0.7 copy.46
  (5 shorter events, 0.1 us)
Async XLA Ops:
  0.6 43.4 %copy-start = (bf16[1,16,128,128]{3,2,1,0:T(8,128)(2,1)S(1)}, bf16[1,16,128,128]{3,2,1,0:T(8,128)(2,1)}, u32[]{:S(2)}) copy-start(bf16[1,16,128,128]{3,2,1,0:T(8,128)(2,1)} %param.13) | copy-start | bytes 1572868
  0.6 0.7 copy-start.3
  0.7 15.0 %copy-start.2 = (bf16[1,1,4,2,128,128]{5,4,3,2,1,0:T(8,128)(2,1)S(1)}, bf16[1,1,4,2,128,128]{5,4,3,2,1,0:T(8,128)(2,1)}, u32[]{:S(2)}) copy-start(bf16[1,1,4,2,128,128]{5,4,3,2,1,0:T(8,128)(2,1)} %param.21) | copy-start | bytes 786436
  0.7 15.2 %copy-start.1 = (bf16[1,1,8,2,128,128]{5,4,3,2,1,0:T(8,128)(2,1)S(1)}, bf16[1,1,8,2,128,128]{5,4,3,2,1,0:T(8,128)(2,1)}, u32[]{:S(2)}) copy-start(bf16[1,1,8,2,128,128]{5,4,3,2,1,0:T(8,128)(2,1)} %param.17) | copy-start | bytes 1572868
  2.0 14.2 %all-to-all-start.2 = ((s32[4,1,2]{2,1,0:T(1,128)}), s32[4,1,2]{2,1,0:T(1,128)S(1)}, u32[]{:S(2)}, u32[]{:S(2)}) async-start(s32[4,1,2]{2,1,0:T(1,128)} %copy.41), calls=%async_computation.2 | async-start | bytes 4096 | tf_op jit(solution)/shard_map/all_to_all | solution.py:65
  16.2 8.3 %all-to-all-start = ((s32[8,1,2]{2,1,0:T(1,128)}), s32[8,1,2]{2,1,0:T(1,128)S(1)}, u32[]{:S(2)}, u32[]{:S(2)}) async-start(s32[8,1,2]{2,1,0:T(1,128)} %copy.36), calls=%async_computation | async-start | bytes 8192 | tf_op jit(solution)/shard_map/all_to_all | solution.py:55
  24.5 10.8 %all-to-all-start.3 = ((f32[4,2,12,128]{3,1,2,0:T(2,128)}), f32[4,2,12,128]{3,1,2,0:T(2,128)S(1)}, u32[]{:S(2)}, u32[]{:S(2)}) async-start(f32[4,2,12,128]{3,1,2,0:T(2,128)} %copy.43), calls=%async_computation.3 | async-start | bytes 98304 | tf_op jit(solution)/shard_map/all_to_all | solution.py:58
  35.3 8.5 %all-to-all-start.1 = ((f32[8,2,12,128]{3,1,2,0:T(2,128)}), f32[8,2,12,128]{3,1,2,0:T(2,128)S(1)}, u32[]{:S(2)}, u32[]{:S(2)}) async-start(f32[8,2,12,128]{3,1,2,0:T(2,128)} %copy.38), calls=%async_computation.1 | async-start | bytes 196608 | tf_op jit(solution)/shard_map/all_to_all | solution.py:52
where the time goes:
time: 84.7 us; the launch traced here: 84.1 us
  blocking collectives  38.5 us (45%)
  starting transfers between devices  18.5 us (22%)
  waiting for transfers between devices  11.2 us (13%)
  local copies, waits for them, and re-layouts  8.43 us (10%)
  other arithmetic  5.33 us (6%)
  matrix products  1.38 us (2%)
    psum x1, blocking collectives, body(): sums = lax.psum(jnp.sum(remapped, axis=(0, 2)), ('level', 'dev'))  38.5 us
    all_to_all x1, starting transfers between devices, body(): lax.all_to_all(left_target[0, 0], 'level', split_axis=0, concat_axis=0, t...  6.35 us
    all_to_all x1, starting transfers between devices, body(): lax.all_to_all(apply_weights(strays, left_weight[0, 0]), 'level', split_a...  5.09 us
    all_to_all x1, waiting for transfers between devices, body(): lax.all_to_all(apply_weights(donors, send_weight[0, 0]), 'dev', split_axi...  4.79 us
    all_to_all x1, waiting for transfers between devices, body(): lax.all_to_all(send_target[0, 0], 'dev', split_axis=0, concat_axis=0, til...  3.97 us
    all_to_all x1, starting transfers between devices, body(): lax.all_to_all(send_target[0, 0], 'dev', split_axis=0, concat_axis=0, til...  3.74 us
    all_to_all x1, starting transfers between devices, body(): lax.all_to_all(apply_weights(donors, send_weight[0, 0]), 'dev', split_axi...  3.36 us
    all_to_all x1, waiting for transfers between devices, body(): lax.all_to_all(apply_weights(strays, left_weight[0, 0]), 'level', split_a...  2.42 us
  transfers between devices with their start and end apart: 4, of which 3 were waited for; matrix products, arithmetic and copies ran while one was open for 14% of the time, Pallas kernels for 0%

commit v1 on v0

--- a/solution.py
+++ b/solution.py
@@ -2,6 +2,11 @@
 import jax.numpy as jnp
 from jax import lax
 from jax.sharding import PartitionSpec as P
+
+
+def connect_space(row_data):
+    raw_out = jax.lax.psum(row_data, "dev")
+    return jax.lax.psum(raw_out, "level")
 
 
 def pick_donors(rounded, block_index, count):
@@ -69,7 +74,7 @@
         + place_terms(intra_terms, intra_target, blocks)
         + place_terms(left_terms, left_where, blocks)
     )
-    sums = lax.psum(jnp.sum(remapped, axis=(0, 2)), ("level", "dev"))
+    sums = connect_space(jnp.sum(remapped, axis=(0, 2)))
     totals = sums / (remapped.shape[2] * blocks)
     return (remapped[None], totals)
 

time: 84.7 us -> 67.8 us (0.80)
  blocking collectives: 38.5 us -> 21.6 us
    psum x1 -> x2, blocking collectives: 38.5 us -> 21.6 us  [the longest x1 11.8 us: connect_space(): raw_out = jax.lax.psum(row_data, 'dev')]
  transfers between devices with their start and end apart: 4 -> 4, of which waited for: 3 -> 3; matrix products, arithmetic and copies ran while one was open for 14% -> 18% of each run, Pallas kernels for 0% -> 0%
where the time goes in v1:
time: 67.8 us; the launch traced here: 67.2 us
  blocking collectives  21.6 us (32%)
  starting transfers between devices  18.5 us (27%)
  waiting for transfers between devices  11.2 us (17%)
  local copies, waits for them, and re-layouts  8.47 us (12%)
  other arithmetic  5.33 us (8%)
  matrix products  1.37 us (2%)
  between operations  0.76 us (1%)
    psum x1, blocking collectives, connect_space(): raw_out = jax.lax.psum(row_data, 'dev')  11.8 us
    psum x1, blocking collectives, connect_space(): return jax.lax.psum(raw_out, 'level')  9.76 us
    all_to_all x1, starting transfers between devices, body(): lax.all_to_all(left_target[0, 0], 'level', split_axis=0, concat_axis=0, t...  6.35 us
    all_to_all x1, starting transfers between devices, body(): lax.all_to_all(apply_weights(strays, left_weight[0, 0]), 'level', split_a...  5.09 us
    all_to_all x1, waiting for transfers between devices, body(): lax.all_to_all(apply_weights(donors, send_weight[0, 0]), 'dev', split_axi...  4.79 us
    all_to_all x1, waiting for transfers between devices, body(): lax.all_to_all(send_target[0, 0], 'dev', split_axis=0, concat_axis=0, til...  3.97 us
    all_to_all x1, starting transfers between devices, body(): lax.all_to_all(send_target[0, 0], 'dev', split_axis=0, concat_axis=0, til...  3.74 us
    all_to_all x1, starting transfers between devices, body(): lax.all_to_all(apply_weights(donors, send_weight[0, 0]), 'dev', split_axi...  3.36 us
  transfers between devices with their start and end apart: 4, of which 3 were waited for; matrix products, arithmetic and copies ran while one was open for 18% of the time, Pallas kernels for 0%

profile of v1, /device:TPU:0, one launch (start us, length us, event | category | flops | bytes accessed | tf_op | source)
XLA Modules:
  0.0 67.2 jit_solution(16323190166845679909)
XLA Ops:
  0.6 0.0 copy-start
  0.6 0.0 copy-start.3
  0.7 0.0 copy-start.2
  0.7 0.0 copy-start.1
  0.7 0.7 %copy-done.3 = s32[1,1,4,2]{2,3,1,0:T(2,128)S(1)} copy-done((s32[1,1,4,2]{2,3,1,0:T(2,128)S(1)}, s32[1,1,4,2]{2,3,1,0:T(2,128)}, u32[]{:S(2)}) %copy-start.3) | copy-done | bytes 56
  1.4 0.7 %copy.41 = s32[4,1,2]{2,1,0:T(1,128)} copy(s32[4,1,2]{0,2,1:T(2,128)S(1)} %bitcast.52) | data formatting | bytes 64 | tf_op jit(solution)/shard_map/all_to_all | solution.py:70
  2.1 6.3 %all-to-all-start.2 = ((s32[4,1,2]{2,1,0:T(1,128)}), s32[4,1,2]{2,1,0:T(1,128)S(1)}, u32[]{:S(2)}, u32[]{:S(2)}) async-start(s32[4,1,2]{2,1,0:T(1,128)} %copy.41), calls=%async_computation.2 | async-start | bytes 4096 | tf_op jit(solution)/shard_map/all_to_all | solution.py:70
  8.4 0.7 fusion.21
  9.1 0.7 %iota_compare_fusion.3 = pred[4,2]{1,0:T(4,128)(4,1)S(1)} fusion(s32[4]{0:T(128)} %bitcast.54), kind=kLoop, calls=%fused_computation.32 | loop fusion | flops 8 | bytes 24 | tf_op jit(solution)/shard_map/lt | solution.py:15
  9.8 0.7 %compare_select_fusion.1 = s32[8,2,1]{0,1,2:T(2,128)S(1)} fusion(s32[1,1,8,2]{2,3,1,0:T(2,128)} %param.14), kind=kLoop, calls=%fused_computation.30 | loop fusion | flops 48 | bytes 128 | tf_op jit(solution)/shard_map/select_n | solution.py:13
  10.5 0.7 %iota_compare_fusion.2 = pred[8,2]{1,0:T(8,128)(4,1)S(1)} fusion(s32[8]{0:T(128)} %bitcast.55), kind=kLoop, calls=%fused_computation.25 | loop fusion | flops 16 | bytes 48 | tf_op jit(solution)/shard_map/lt | solution.py:15
  11.2 0.7 %compare_select_fusion = s32[4,2,1]{0,1,2:T(2,128)S(1)} fusion(s32[1,1,4,2]{2,3,1,0:T(2,128)} %param.18), kind=kLoop, calls=%fused_computation.29 | loop fusion | flops 24 | bytes 64 | tf_op jit(solution)/shard_map/select_n | solution.py:13
  11.9 0.1 copy.42
  12.0 0.1 reshape.173
  12.1 0.1 copy.37
  12.1 0.1 reshape.165
  12.2 1.3 %copy.36 = s32[8,1,2]{2,1,0:T(1,128)} copy(s32[8,1,2]{0,2,1:T(2,128)} %bitcast.53) | data formatting | bytes 128 | tf_op jit(solution)/shard_map/all_to_all | solution.py:60
  13.6 0.9 %copy.52 = bf16[1,16,12,128]{3,2,1,0:T(8,128)(2,1)S(1)} copy(f32[1,16,12,128]{3,1,2,0:T(8,128)} %param.11) | data formatting | bytes 147456 | tf_op args[0]
  14.5 0.6 gather_fusion.2
  15.1 0.6 gather_fusion.1
  15.7 0.0 copy-done.2
  15.7 0.2 fusion.4
  15.9 0.0 copy-done.1
  15.9 0.3 fusion.1
  16.2 0.0 all-to-all-done.2
  16.2 3.7 %all-to-all-start = ((s32[8,1,2]{2,1,0:T(1,128)}), s32[8,1,2]{2,1,0:T(1,128)S(1)}, u32[]{:S(2)}, u32[]{:S(2)}) async-start(s32[8,1,2]{2,1,0:T(1,128)} %copy.36), calls=%async_computation | async-start | bytes 8192 | tf_op jit(solution)/shard_map/all_to_all | solution.py:60
  20.0 0.6 copy.43
  20.6 4.0 %all-to-all-done = s32[8,1,2]{2,1,0:T(1,128)S(1)} async-done(((s32[8,1,2]{2,1,0:T(1,128)}), s32[8,1,2]{2,1,0:T(1,128)S(1)}, u32[]{:S(2)}, u32[]{:S(2)}) %all-to-all-start) | async-done | bytes 96 | tf_op jit(solution)/shard_map/all_to_all | solution.py:60
  24.6 5.1 %all-to-all-start.3 = ((f32[4,2,12,128]{3,1,2,0:T(2,128)}), f32[4,2,12,128]{3,1,2,0:T(2,128)S(1)}, u32[]{:S(2)}, u32[]{:S(2)}) async-start(f32[4,2,12,128]{3,1,2,0:T(2,128)} %copy.43), calls=%async_computation.3 | async-start | bytes 98304 | tf_op jit(solution)/shard_map/all_to_all | solution.py:63
  29.7 0.6 gather_fusion
  30.3 0.7 %copy.38 = f32[8,2,12,128]{3,1,2,0:T(2,128)} copy(f32[8,2,12,128]{3,2,1,0:T(8,128)S(1)} %fusion.1) | data formatting | bytes 196608 | tf_op jit(solution)/shard_map/pcmk,pcki->pcmi/dot_general | solution.py:20
  30.9 0.5 broadcast.122
  31.5 0.7 reduce.6
  32.1 0.1 eq.34
  32.2 0.7 reduce.7
  32.9 0.1 eq.30
  33.0 2.4 %all-to-all-done.3 = f32[4,2,12,128]{3,1,2,0:T(2,128)S(1)} async-done(((f32[4,2,12,128]{3,1,2,0:T(2,128)}), f32[4,2,12,128]{3,1,2,0:T(2,128)S(1)}, u32[]{:S(2)}, u32[]{:S(2)}) %all-to-all-start.3) | async-done | bytes 49184 | tf_op jit(solution)/shard_map/all_to_all | solution.py:63
  35.4 3.4 %all-to-all-start.1 = ((f32[8,2,12,128]{3,1,2,0:T(2,128)}), f32[8,2,12,128]{3,1,2,0:T(2,128)S(1)}, u32[]{:S(2)}, u32[]{:S(2)}) async-start(f32[8,2,12,128]{3,1,2,0:T(2,128)} %copy.38), calls=%async_computation.1 | async-start | bytes 196608 | tf_op jit(solution)/shard_map/all_to_all | solution.py:57
  38.8 0.3 fusion.18
  39.1 4.8 %all-to-all-done.1 = f32[8,2,12,128]{3,1,2,0:T(2,128)S(1)} async-done(((f32[8,2,12,128]{3,1,2,0:T(2,128)}), f32[8,2,12,128]{3,1,2,0:T(2,128)S(1)}, u32[]{:S(2)}, u32[]{:S(2)}) %all-to-all-start.1) | async-done | bytes 98336 | tf_op jit(solution)/shard_map/all_to_all | solution.py:57
  43.9 0.2 fusion.14
  44.1 0.0 copy-done
  44.1 0.4 fusion.24
  44.5 11.8 %psum.14 = f32[12]{0:T(128)S(1)} all-reduce(f32[12]{0:T(128)S(1)} %get-tuple-element.8), channel_id=1, replica_groups=mesh['level'=4,'dev'=8] {'dev'}, use_global_device_ids=true, to_apply=%region_1.2 | all-reduce | flops 12 | bytes 96 | tf_op jit(solution)/shard_map/psum | solution.py:8
  56.3 9.8 %psum.15 = f32[12]{0:T(128)S(1)} all-reduce(f32[12]{0:T(128)S(1)} %psum.14), channel_id=1, replica_groups=mesh['level'=4,'dev'=8] {'level'}, use_global_device_ids=true, to_apply=%region_2.3 | all-reduce | flops 12 | bytes 96 | tf_op jit(solution)/shard_map/psum | solution.py:9
  66.0 0.5 broadcast_multiply_fusion
  66.6 0.7 copy.46
  (5 shorter events, 0.1 us)
Async XLA Ops:
  0.6 43.5 %copy-start = (bf16[1,16,128,128]{3,2,1,0:T(8,128)(2,1)S(1)}, bf16[1,16,128,128]{3,2,1,0:T(8,128)(2,1)}, u32[]{:S(2)}) copy-start(bf16[1,16,128,128]{3,2,1,0:T(8,128)(2,1)} %param.13) | copy-start | bytes 1572868
  0.6 0.7 %copy-start.3 = (s32[1,1,4,2]{2,3,1,0:T(2,128)S(1)}, s32[1,1,4,2]{2,3,1,0:T(2,128)}, u32[]{:S(2)}) copy-start(s32[1,1,4,2]{2,3,1,0:T(2,128)} %param.19) | copy-start | bytes 100
  0.7 15.0 %copy-start.2 = (bf16[1,1,4,2,128,128]{5,4,3,2,1,0:T(8,128)(2,1)S(1)}, bf16[1,1,4,2,128,128]{5,4,3,2,1,0:T(8,128)(2,1)}, u32[]{:S(2)}) copy-start(bf16[1,1,4,2,128,128]{5,4,3,2,1,0:T(8,128)(2,1)} %param.21) | copy-start | bytes 786436
  0.7 15.2 %copy-start.1 = (bf16[1,1,8,2,128,128]{5,4,3,2,1,0:T(8,128)(2,1)S(1)}, bf16[1,1,8,2,128,128]{5,4,3,2,1,0:T(8,128)(2,1)}, u32[]{:S(2)}) copy-start(bf16[1,1,8,2,128,128]{5,4,3,2,1,0:T(8,128)(2,1)} %param.17) | copy-start | bytes 1572868
  2.1 14.2 %all-to-all-start.2 = ((s32[4,1,2]{2,1,0:T(1,128)}), s32[4,1,2]{2,1,0:T(1,128)S(1)}, u32[]{:S(2)}, u32[]{:S(2)}) async-start(s32[4,1,2]{2,1,0:T(1,128)} %copy.41), calls=%async_computation.2 | async-start | bytes 4096 | tf_op jit(solution)/shard_map/all_to_all | solution.py:70
  16.2 8.3 %all-to-all-start = ((s32[8,1,2]{2,1,0:T(1,128)}), s32[8,1,2]{2,1,0:T(1,128)S(1)}, u32[]{:S(2)}, u32[]{:S(2)}) async-start(s32[8,1,2]{2,1,0:T(1,128)} %copy.36), calls=%async_computation | async-start | bytes 8192 | tf_op jit(solution)/shard_map/all_to_all | solution.py:60
  24.6 10.8 %all-to-all-start.3 = ((f32[4,2,12,128]{3,1,2,0:T(2,128)}), f32[4,2,12,128]{3,1,2,0:T(2,128)S(1)}, u32[]{:S(2)}, u32[]{:S(2)}) async-start(f32[4,2,12,128]{3,1,2,0:T(2,128)} %copy.43), calls=%async_computation.3 | async-start | bytes 98304 | tf_op jit(solution)/shard_map/all_to_all | solution.py:63
  35.4 8.5 %all-to-all-start.1 = ((f32[8,2,12,128]{3,1,2,0:T(2,128)}), f32[8,2,12,128]{3,1,2,0:T(2,128)S(1)}, u32[]{:S(2)}, u32[]{:S(2)}) async-start(f32[8,2,12,128]{3,1,2,0:T(2,128)} %copy.38), calls=%async_computation.1 | async-start | bytes 196608 | tf_op jit(solution)/shard_map/all_to_all | solution.py:57
